TPU v7x, 32 devices: a whole 2x2x4 slice. The times are simulated.
32 devices in a mesh: dp: 4 (over y, x), head: 4 (over z), ctx: 2 (over core).
Axes of the slice: x: 2, y: 2, z: 4, core: 2. Of those that a mesh axis runs over, the one named last changes fastest.
Arguments:
- tokens: bfloat16 [8192, 768], P(('dp', 'head', 'ctx')), may hold values from -6 to 6
- cotangent: bfloat16 [8192, 768], P(('dp', 'head', 'ctx')), may hold values from -6 to 6
- in_master: float32 [768, 3968], P('head'), may hold values from -4 to 4
- in_moment: float32 [768, 3968], P('head'), may hold values from -245760 to 245760
- in_second: float32 [768, 3968], P('head'), may hold values from 0 to 8192000, as said below
- out_master: float32 [3840, 768], P('head'), may hold values from -4 to 4
- out_moment: float32 [3840, 768], P('head'), may hold values from -245760 to 245760
- out_second: float32 [3840, 768], P('head'), may hold values from 0 to 8192000, as said below
- vec_master: float32 [7808], replicated, may hold values from -4 to 4
- vec_moment: float32 [7808], replicated, may hold values from -245760 to 245760
- vec_second: float32 [7808], replicated, may hold values from 0 to 8192000, as said below
- rotary_scale: int32 [1], replicated, may hold values from 2 to 8
Outputs:
- output: bfloat16 [8192, 768], P(('dp', 'head', 'ctx'))
- input_grad: bfloat16 [8192, 768], P(('dp', 'head', 'ctx'))
- in_moment_new: float32 [768, 3968], P('head')
- in_second_new: float32 [768, 3968], P('head')
- in_master_new: float32 [768, 3968], P('head')
- in_copy: bfloat16 [768, 3968], P('head')
- out_moment_new: float32 [3840, 768], P('head')
- out_second_new: float32 [3840, 768], P('head')
- out_master_new: float32 [3840, 768], P('head')
- out_copy: bfloat16 [3840, 768], P('head')
- vec_moment_new: float32 [7808], replicated
- vec_second_new: float32 [7808], replicated
- vec_master_new: float32 [7808], replicated
Inputs may be any that keep to these rules, and one draw needn't show every extreme that they name: `in_second`: positive entries. `out_second`: positive entries. `vec_second`: positive entries.
All inputs are finite; a program needn't handle non-finite values.
Results may differ from a plain program's by a relative error of at most 0.014.
The roundings to bfloat16 on the way count: a program that leaves them out, or rounds other values in their place, can miss the bound.
Values may be sent and summed in bfloat16 or wider, within the bound.
A program may use at most 192 MiB of HBM per device.

v0:
```python
import jax
import jax.numpy as jnp
from jax import lax
from jax.sharding import PartitionSpec as P

HEADS = 12
HEAD_DIM = 64
ROT = 16
D = 768
KEY_BLOCK = 1024
ADAM_STEP = 3


neg_fill = -1e30
matrix_rate = 0.03
vector_rate = 0.3
weight_decay = 0.1
adam_epsilon = 1e-08
contract_rows = (((0,), (0,)), ((), ()))
contract_cols = (((1,), (1,)), ((), ()))


def layer_norm(values, norm_gain, norm_shift):
    center = values - jnp.mean(values, axis=-1, keepdims=True)
    inverse = lax.rsqrt(jnp.mean(center * center, axis=-1, keepdims=True) + 1e-05)
    normed = center * inverse
    return (normed * norm_gain + norm_shift, normed, inverse)


def norm_back(upstream, normed, inverse, norm_gain):
    scaled = upstream * norm_gain
    inside = (
        scaled
        - jnp.mean(scaled, axis=-1, keepdims=True)
        - normed * jnp.mean(scaled * normed, axis=-1, keepdims=True)
    )
    return (inverse * inside, jnp.sum(upstream * normed, axis=0), jnp.sum(upstream, axis=0))


def rotary_tables(positions, scale_value):
    half_rot = ROT // 2
    frequency = 10000.0 ** (-(2.0 * jnp.arange(half_rot, dtype=jnp.float32)) / ROT)
    angles = (positions / scale_value)[:, None] * frequency[None, :]
    return (jnp.cos(angles), jnp.sin(angles))


def rotate(values, cosine, sine_table):
    half_rot = ROT // 2
    front_half = values[..., :half_rot]
    back_half = values[..., half_rot:ROT]
    return jnp.concatenate(
        [
            front_half * cosine - back_half * sine_table,
            back_half * cosine + front_half * sine_table,
            values[..., ROT:],
        ],
        axis=-1,
    )


def score_block(query_rows, row_pos, whole_kv, block_index):
    key_block = lax.dynamic_slice_in_dim(whole_kv, block_index * KEY_BLOCK, KEY_BLOCK, 0)
    scores = lax.dot_general(
        query_rows, key_block[:, :HEAD_DIM], contract_cols, preferred_element_type=jnp.float32
    )
    key_pos = block_index * KEY_BLOCK + jnp.arange(KEY_BLOCK, dtype=jnp.int32)
    allowed = key_pos[None, :] <= row_pos[:, None]
    return (jnp.where(allowed, scores, neg_fill), allowed, key_block)


def log_totals(query_rows, row_pos, whole_kv):
    row_count = query_rows.shape[0]
    last_pos = jnp.max(row_pos)

    def advance(block_index, state_now):

        def process(state_old):
            run_max, run_sum = state_old
            scores, allowed, key_block = score_block(query_rows, row_pos, whole_kv, block_index)
            new_max = jnp.maximum(run_max, jnp.max(scores, axis=1))
            weights = jnp.where(allowed, jnp.exp(scores - new_max[:, None]), 0.0)
            return (new_max, run_sum * jnp.exp(run_max - new_max) + jnp.sum(weights, axis=1))

        return lax.cond(
            block_index * KEY_BLOCK <= last_pos, process, lambda state_same: state_same, state_now
        )

    start_state = (
        jnp.full((row_count,), neg_fill, jnp.float32),
        jnp.zeros((row_count,), jnp.float32),
    )
    run_max, run_sum = lax.fori_loop(0, whole_kv.shape[0] // KEY_BLOCK, advance, start_state)
    return run_max + jnp.log(run_sum)


def attend(query_rows, row_pos, whole_kv, log_sum):
    last_pos = jnp.max(row_pos)

    def advance(block_index, summed):

        def process(summed_old):
            scores, allowed, key_block = score_block(query_rows, row_pos, whole_kv, block_index)
            probs = jnp.where(allowed, jnp.exp(scores - log_sum[:, None]), 0.0).astype(jnp.bfloat16)
            return summed_old + jnp.dot(
                probs, key_block[:, HEAD_DIM:], preferred_element_type=jnp.float32
            )

        return lax.cond(
            block_index * KEY_BLOCK <= last_pos, process, lambda summed_same: summed_same, summed
        )

    start_state = jnp.zeros((query_rows.shape[0], HEAD_DIM), jnp.float32)
    return lax.fori_loop(0, whole_kv.shape[0] // KEY_BLOCK, advance, start_state)


def attend_back(query_rows, row_pos, whole_kv, log_sum, grad_rows, row_inner):
    last_pos = jnp.max(row_pos)

    def advance(block_index, state_now):

        def process(state_old):
            query_grad, kv_terms = state_old
            scores, allowed, key_block = score_block(query_rows, row_pos, whole_kv, block_index)
            probs = jnp.where(allowed, jnp.exp(scores - log_sum[:, None]), 0.0)
            prob_grad = lax.dot_general(
                grad_rows,
                key_block[:, HEAD_DIM:],
                contract_cols,
                preferred_element_type=jnp.float32,
            )
            score_grad = (probs * (prob_grad - row_inner[:, None])).astype(jnp.bfloat16)
            query_grad = query_grad + jnp.dot(
                score_grad, key_block[:, :HEAD_DIM], preferred_element_type=jnp.float32
            )
            key_grad = lax.dot_general(
                score_grad, query_rows, contract_rows, preferred_element_type=jnp.float32
            )
            value_grad = lax.dot_general(
                probs.astype(jnp.bfloat16),
                grad_rows,
                contract_rows,
                preferred_element_type=jnp.float32,
            )
            kv_terms = lax.dynamic_update_slice_in_dim(
                kv_terms,
                jnp.concatenate([key_grad, value_grad], axis=1),
                block_index * KEY_BLOCK,
                0,
            )
            return (query_grad, kv_terms)

        return lax.cond(
            block_index * KEY_BLOCK <= last_pos, process, lambda state_same: state_same, state_now
        )

    start_state = (
        jnp.zeros((query_rows.shape[0], HEAD_DIM), jnp.float32),
        jnp.zeros((whole_kv.shape[0], 2 * HEAD_DIM), jnp.float32),
    )
    return lax.fori_loop(0, whole_kv.shape[0] // KEY_BLOCK, advance, start_state)


def adam_update(master, moment, second, gradient, step_rate, decay_rate):
    moment_new = 0.5 * moment + 0.5 * gradient
    second_new = 0.5 * second + 0.5 * gradient * gradient
    correction = 1.0 - 0.5**ADAM_STEP
    normalized = moment_new / correction / (jnp.sqrt(second_new / correction) + adam_epsilon)
    return (moment_new, second_new, master - step_rate * (normalized + decay_rate * master))


def shards(
    tokens,
    cotangent,
    in_master,
    in_moment,
    in_second,
    out_master,
    out_moment,
    out_second,
    vec_master,
    vec_moment,
    vec_second,
    rotary_scale,
):
    local_rows = tokens.shape[0]
    full_in, full_out = (
        lax.all_gather(in_master.astype(jnp.bfloat16), "head", axis=0, tiled=True),
        lax.all_gather(out_master.astype(jnp.bfloat16), "head", axis=0, tiled=True),
    )
    scale_value = rotary_scale[0].astype(jnp.float32)
    local_pos = lax.axis_index(("head", "ctx")) * local_rows + jnp.arange(
        local_rows, dtype=jnp.int32
    )
    cosine, sine_table = rotary_tables(local_pos.astype(jnp.float32), scale_value)
    inputs = tokens.astype(jnp.float32)
    norm_one, normed_one, inverse_one = layer_norm(inputs, vec_master[0:D], vec_master[D : 2 * D])
    norm_two, normed_two, inverse_two = layer_norm(
        inputs, vec_master[2 * D : 3 * D], vec_master[3 * D : 4 * D]
    )
    first_in = norm_one.astype(jnp.bfloat16)
    second_in = norm_two.astype(jnp.bfloat16)
    projected = (
        jnp.dot(first_in, full_in[:, : D + 2 * HEAD_DIM], preferred_element_type=jnp.float32)
        + vec_master[5 * D : 6 * D + 2 * HEAD_DIM]
    )
    hidden_in = (
        jnp.dot(second_in, full_in[:, D + 2 * HEAD_DIM :], preferred_element_type=jnp.float32)
        + vec_master[6 * D + 2 * HEAD_DIM :]
    )
    query_heads = projected[:, :D].reshape(local_rows, HEADS, HEAD_DIM)
    queries = (
        (rotate(query_heads, cosine[:, None, :], sine_table[:, None, :]) * 0.125)
        .astype(jnp.bfloat16)
        .reshape(local_rows, D)
    )
    key_part = rotate(projected[:, D : D + HEAD_DIM], cosine, sine_table)
    shared = jnp.concatenate([key_part, projected[:, D + HEAD_DIM :]], axis=1).astype(jnp.bfloat16)
    whole_kv = lax.all_gather(shared, ("head", "ctx"), axis=0, tiled=True)
    activated = jax.nn.gelu(hidden_in, approximate=False).astype(jnp.bfloat16)
    heads_here = queries.shape[1] // HEAD_DIM
    query_rows = queries.reshape(-1, HEAD_DIM)
    row_pos = jnp.repeat(local_pos, heads_here)
    log_sum = log_totals(query_rows, row_pos, whole_kv)
    attended = attend(query_rows, row_pos, whole_kv, log_sum)
    att_out = attended.reshape(queries.shape).astype(jnp.bfloat16)
    branch_pair = jnp.concatenate([att_out, activated], axis=1)
    output = (
        inputs
        + jnp.dot(branch_pair, full_out, preferred_element_type=jnp.float32)
        + vec_master[4 * D : 5 * D]
    ).astype(jnp.bfloat16)
    cot_in = cotangent.astype(jnp.float32)
    grad_out = lax.dot_general(
        branch_pair, cotangent, contract_rows, preferred_element_type=jnp.float32
    )
    back_proj = lax.dot_general(
        cotangent, full_out, contract_cols, preferred_element_type=jnp.float32
    )
    branch_grad = back_proj[:, :D].astype(jnp.bfloat16)
    gelu_back = jax.vjp(lambda pre_act: jax.nn.gelu(pre_act, approximate=False), hidden_in)[1]
    hidden_grad = gelu_back(back_proj[:, D:])[0].astype(jnp.bfloat16)
    grad_rows = branch_grad.reshape(-1, HEAD_DIM)
    row_inner = jnp.sum(grad_rows.astype(jnp.float32) * attended, axis=1)
    query_grad, kv_terms = attend_back(query_rows, row_pos, whole_kv, log_sum, grad_rows, row_inner)
    att_cos, att_sin = rotary_tables(local_pos.astype(jnp.float32), scale_value)
    query_pre = rotate(
        query_grad.reshape(-1, heads_here, HEAD_DIM) * 0.125,
        att_cos[:, None, :],
        -att_sin[:, None, :],
    )
    query_pre = query_pre.reshape(queries.shape).astype(jnp.bfloat16)
    kv_sum = lax.psum_scatter(kv_terms, ("head", "ctx"), scatter_dimension=0, tiled=True)
    shared_grad = jnp.concatenate(
        [rotate(kv_sum[:, :HEAD_DIM], cosine, -sine_table), kv_sum[:, HEAD_DIM:]], axis=1
    ).astype(jnp.bfloat16)
    attn_grad = jnp.concatenate([query_pre, shared_grad], axis=1)
    grad_in = jnp.concatenate(
        [
            lax.dot_general(first_in, attn_grad, contract_rows, preferred_element_type=jnp.float32),
            lax.dot_general(
                second_in, hidden_grad, contract_rows, preferred_element_type=jnp.float32
            ),
        ],
        axis=1,
    )
    norm_grad_one = lax.dot_general(
        attn_grad, full_in[:, : D + 2 * HEAD_DIM], contract_cols, preferred_element_type=jnp.float32
    )
    norm_grad_two = lax.dot_general(
        hidden_grad,
        full_in[:, D + 2 * HEAD_DIM :],
        contract_cols,
        preferred_element_type=jnp.float32,
    )
    input_one, gain_one, shift_one = norm_back(
        norm_grad_one, normed_one, inverse_one, vec_master[0:D]
    )
    input_two, gain_two, shift_two = norm_back(
        norm_grad_two, normed_two, inverse_two, vec_master[2 * D : 3 * D]
    )
    input_grad = (cot_in + input_one + input_two).astype(jnp.bfloat16)
    grad_vec = jnp.concatenate(
        [
            gain_one,
            shift_one,
            gain_two,
            shift_two,
            jnp.sum(cot_in, axis=0),
            jnp.sum(attn_grad.astype(jnp.float32), axis=0),
            jnp.sum(hidden_grad.astype(jnp.float32), axis=0),
        ]
    )
    shard_in, shard_out = (
        lax.psum_scatter(
            grad_in.astype(jnp.bfloat16), "head", scatter_dimension=0, tiled=True
        ).astype(jnp.float32),
        lax.psum_scatter(
            grad_out.astype(jnp.bfloat16), "head", scatter_dimension=0, tiled=True
        ).astype(jnp.float32),
    )
    summed_in, summed_out = lax.psum((shard_in, shard_out), ("dp", "ctx"))
    summed_vec = lax.psum(grad_vec, ("dp", "head", "ctx"))
    in_moment_new, in_second_new, in_master_new = adam_update(
        in_master, in_moment, in_second, summed_in, matrix_rate, weight_decay
    )
    out_moment_new, out_second_new, out_master_new = adam_update(
        out_master, out_moment, out_second, summed_out, matrix_rate, weight_decay
    )
    vec_moment_new, vec_second_new, vec_master_new = adam_update(
        vec_master, vec_moment, vec_second, summed_vec, vector_rate, 0.0
    )
    return (
        output,
        input_grad,
        in_moment_new,
        in_second_new,
        in_master_new,
        in_master_new.astype(jnp.bfloat16),
        out_moment_new,
        out_second_new,
        out_master_new,
        out_master_new.astype(jnp.bfloat16),
        vec_moment_new,
        vec_second_new,
        vec_master_new,
    )


def solution(mesh):
    placed = (
        P(("dp", "head", "ctx"), None),
        P(("dp", "head", "ctx"), None),
        P("head", None),
        P("head", None),
        P("head", None),
        P("head", None),
        P("head", None),
        P("head", None),
        P(),
        P(),
        P(),
        P(),
    )
    return jax.shard_map(
        shards,
        mesh=mesh,
        in_specs=placed,
        out_specs=(
            P(("dp", "head", "ctx"), None),
            P(("dp", "head", "ctx"), None),
            P("head", None),
            P("head", None),
            P("head", None),
            P("head", None),
            P("head", None),
            P("head", None),
            P("head", None),
            P("head", None),
            P(),
            P(),
            P(),
        ),
        check_vma=False,
    )
```

profile of v0, /device:TPU:0, one launch (start us, length us, event | category | flops | bytes accessed | tf_op | source)
XLA Modules:
  0.0 735.1 jit_solution(5293587416853408413)
XLA Ops:
  7.2 3.1 convert_element_type.127
  10.4 3.2 convert_element_type.118
  16.7 105.3 %all-gather.5.cloned.1.call-done = bf16[3840,768]{1,0:T(8,128)(2,1)} async-done(((bf16[960,768]{1,0:T(8,128)(2,1)}), bf16[3840,768]{1,0:T(8,128)(2,1)}) %all-gather.5.cloned.1.call-update) | async-done | bytes 5898256 | tf_op jit(solution)/shard_map/all_gather | solution.py:188
  122.1 4.4 fusion.114
  129.8 104.8 %all-gather.3.cloned.1.call-done = bf16[768,3968]{1,0:T(8,128)(2,1)} async-done(((bf16[192,3968]{1,0:T(8,128)(2,1)}), bf16[768,3968]{1,0:T(8,128)(2,1)}) %all-gather.3.cloned.1.call-update) | async-done | bytes 6094864 | tf_op jit(solution)/shard_map/all_gather | solution.py:187
  237.6 14.8 %all_gather.10 = bf16[2048,128]{0,1:T(8,128)(2,1)S(1)} all-gather(bf16[256,128]{0,1:T(8,128)(2,1)S(1)} %pad_maximum_fusion.12), channel_id=1, replica_groups=mesh['dp'=4,'head'=4,'ctx'=2] {'head','ctx'}, dimensions={0}, use_global_device_ids=true | all-gather | bytes 589824 | tf_op jit(solution)/shard_map/all_gather | solution.py:218
  267.0 2.8 fusion.50
  269.8 6.9 while.49
  270.6 5.5 conditional.9
  272.7 3.4 fusion.6
  276.8 5.4 while.50
  277.4 4.1 conditional.10
  277.7 3.9 convolution_add_fusion
  286.9 23.4 %while.51 = (s32[]{:T(128)}, f32[3072,64]{0,1:T(8,128)S(1)}, f32[2048,128]{0,1:T(8,128)}, s32[]{:T(128)}, bf16[2048,128]{1,0:T(8,128)(2,1)S(1)}, /*index=5*/bf16...) while((s32[]{:T(128)}, f32[3072,64]{0,1:T(8,128)S(1)}, ...), condition=%wide.region_17.18_spmd.clone, body=%wide.region_14.17_spmd.clone.sunk | while | flops 2051343360 | bytes 122926544 | solution.py:160
  287.7 22.0 %conditional.11 = ((f32[3072,64]{0,1:T(8,128)S(1)}, f32[2048,128]{0,1:T(8,128)})) conditional(s32[]{:T(128)} %convert_element_type.243, (f32[3072,64]{0,1:T(8,128)S(1)}, f32[2048,128]{0,1:T(8,128)}) %tuple.169, (s32[]{:T(128)}, s32[256]{0:T(256)S(1)}, bf16[2048,128]{1,0:T(8,128)(2,1)S(1)}, bf16[3072,64]{1,0:T(8,128)(2,1)S(1)}, ...), branch_computations={%region_15.15_spmd, %region_16.16_spmd} | conditional | flops 2051343360 | bytes 122926304 | solution.py:152
  287.7 6.3 fusion.29
  294.3 8.3 %fusion.23 = bf16[3072,1024]{0,1:T(8,128)(2,1)S(1)} fusion(f32[1024,3072]{1,0:T(8,128)} %fusion.29, bf16[3072,64]{1,0:T(8,128)(2,1)} %get-tuple-element.489, f32[3072]{0:T(1024)S(1)} %get-tuple-element.490, f32[3072]{0:T(1024)S(1)} %get-tuple-element.488, s32[3072]{0:T(1024)S(1)} %le.62, s32[1024]{0:T(1024)S(1)} %iota_add_fusion.2, ...), kind=kOutput, calls=%fused_computation.29 | convolution fusion | flops 424673280 | bytes 19570696 | tf_op jit(solution)/shard_map/while/body/eval_jaxpr/cond/branch_1_fun/dot_general | solution.py:125
  304.0 2.7 fusion.25
  310.5 13.2 %convert_reduce_fusion = (f32[3072]{0:T(1024)S(1)}, bf16[256,3072]{1,0:T(8,128)(2,1)}, f32[256,3072]{1,0:T(8,128)}, f32[256,3072]{1,0:T(8,128)}) fusion(f32[256,3840]{1,0:T(8,128)} %copy-done.28, f32[3072]{0:T(1024)S(1)} %copy-done.38, bf16[768,3968]{1,0:T(8,128)(2,1)} %all-gather.3.cloned.1.call-done, bf16[256,768]{1,0:T(8,128)(2,1)S(1)} %copy-done.4, ...), kind=kOutput, calls=%fused_computation.57 | convolution fusion | flops 1268118528 | bytes 16154624 | tf_op jit(solution)/shard_map/dot_general | solution.py:207
  324.6 3.5 multiply_convert_fusion
  329.3 4.3 convolution_convert_fusion
  348.7 5.1 convolution_convert_fusion.1
  353.8 19.2 %reduce-scatter.4.cloned.1.call-done = f32[256,128]{0,1:T(8,128)} async-done(((f32[2048,128]{0,1:T(8,128)}), f32[256,128]{0,1:T(8,128)}) %reduce-scatter.4.cloned.1.call-update) | async-done | bytes 131088 | tf_op jit(solution)/shard_map/reduce_scatter | solution.py:252
  375.5 5.9 pad_maximum_fusion
  382.8 3.9 fusion.35
  386.8 5.1 fusion.54
  396.0 58.5 %psum.23 = f32[7808]{0:T(1024)S(1)} all-reduce(f32[7808]{0:T(1024)S(1)} %constant_dynamic-update-slice_fusion), channel_id=1, replica_groups=mesh['dp'=4,'head'=4,'ctx'=2] {'dp','head','ctx'}, use_global_device_ids=true, to_apply=%region_34.35 | all-reduce | flops 7808 | bytes 62464 | tf_op jit(solution)/shard_map/psum | solution.py:302
  455.2 24.1 %reduce-scatter.8.cloned.1.call-done = bf16[960,768]{1,0:T(8,128)(2,1)} async-done(((bf16[3840,768]{1,0:T(8,128)(2,1)}), bf16[960,768]{1,0:T(8,128)(2,1)}) %reduce-scatter.8.cloned.1.call-update) | async-done | bytes 1474576 | tf_op jit(solution)/shard_map/reduce_scatter | solution.py:297
  479.3 110.2 %reduce-scatter.6.cloned.1.call-done = bf16[192,3968]{1,0:T(8,128)(2,1)} async-done(((bf16[768,3968]{1,0:T(8,128)(2,1)}), bf16[192,3968]{1,0:T(8,128)(2,1)}) %reduce-scatter.6.cloned.1.call-update) | async-done | bytes 1523728 | tf_op jit(solution)/shard_map/reduce_scatter | solution.py:294
  589.5 123.2 %all-reduce.2 = (f32[192,3968]{1,0:T(8,128)}, f32[960,768]{1,0:T(8,128)S(1)}) all-reduce(bf16[192,3968]{1,0:T(8,128)(2,1)} %reduce-scatter.6.cloned.1.call-done, bf16[960,768]{1,0:T(8,128)(2,1)} %reduce-scatter.8.cloned.1.call-done), channel_id=1, replica_groups=mesh['dp'=4,'head'=4,'ctx'=2] {'dp','ctx'}, use_global_device_ids=true, to_apply=%region_24.25 | all-reduce | flops 1499136 | bytes 8994816 | tf_op jit(solution)/shard_map/psum | solution.py:301
  712.8 8.7 %fusion.109 = (bf16[192,3968]{1,0:T(8,128)(2,1)}, f32[192,3968]{1,0:T(8,128)}, f32[192,3968]{1,0:T(8,128)}, f32[192,3968]{1,0:T(8,128)}) fusion(f32[192,3968]{1,0:T(8,128)} %param.26, f32[192,3968]{1,0:T(8,128)} %get-tuple-element.700, f32[192,3968]{1,0:T(8,128)} %param.28, f32[192,3968]{1,0:T(8,128)} %param.27), kind=kLoop, calls=%fused_computation.176 | loop fusion | flops 11427840 | bytes 22855680 | tf_op jit(solution)/shard_map/convert_element_type | solution.py:318
  723.6 4.8 fusion.107
  (188 shorter events, 62.8 us)
Async XLA Ops:
  7.2 114.9 %all-gather.5.cloned.1.call-start = ((), (), s32[]{:S(2)}) async-start(), calls=%async_computation.4 | async-start | bytes 7372800 | tf_op jit(solution)/shard_map/all_gather | solution.py:188
  10.4 111.7 %copy-start.17 = (bf16[256,768]{1,0:T(8,128)(2,1)S(1)}, bf16[256,768]{1,0:T(8,128)(2,1)}, u32[]{:S(2)}) copy-start(bf16[256,768]{1,0:T(8,128)(2,1)} %param.25) | copy-start | bytes 1179652
  10.4 224.2 %all-gather.3.cloned.1.call-start = ((), (), s32[]{:S(2)}) async-start(), calls=%async_computation.3 | async-start | bytes 7618560 | tf_op jit(solution)/shard_map/all_gather | solution.py:187
  13.7 359.3 %reduce-scatter.4.cloned.1.call-start = ((), (), s32[]{:S(2)}) async-start(), calls=%async_computation.5 | async-start | bytes 1179648 | tf_op jit(solution)/shard_map/reduce_scatter | solution.py:252
  15.0 221.8 %copy-start.44 = (f32[8]{0:T(128)}, f32[8]{0:T(128)S(1)}, u32[]{:S(2)}) copy-start(f32[8]{0:T(128)S(1)} %multiply_power_fusion) | copy-start | bytes 100
  15.0 221.8 %copy-start.39 = (f32[256]{0:T(256)}, f32[256]{0:T(256)S(1)}, u32[]{:S(2)}) copy-start(f32[256]{0:T(256)S(1)} %convert_divide_fusion) | copy-start | bytes 3076
  15.8 218.7 %copy-start.32 = (f32[256]{0:T(256)}, f32[256]{0:T(256)S(1)}, u32[]{:S(2)}) copy-start(f32[256]{0:T(256)S(1)} %broadcast_multiply_fusion.5) | copy-start | bytes 3076
  16.1 218.5 %copy-start.36 = (f32[256]{0:T(256)}, f32[256]{0:T(256)S(1)}, u32[]{:S(2)}) copy-start(f32[256]{0:T(256)S(1)} %add_rsqrt_fusion) | copy-start | bytes 3076
  16.7 217.9 %copy-start.34 = (f32[768]{0:T(1024)}, f32[768]{0:T(1024)S(1)}, u32[]{:S(2)}) copy-start(f32[768]{0:T(1024)S(1)} %get-tuple-element.734) | copy-start | bytes 9220
  16.7 217.9 %copy-start.42 = (f32[768]{0:T(1024)}, f32[768]{0:T(1024)S(1)}, u32[]{:S(2)}) copy-start(f32[768]{0:T(1024)S(1)} %get-tuple-element.733) | copy-start | bytes 9220
  237.6 19.7 %copy-start.26 = (f32[256,8]{0,1:T(8,128)}, f32[256,8]{0,1:T(8,128)S(1)}, u32[]{:S(2)}) copy-start(f32[256,8]{0,1:T(8,128)S(1)} %get-tuple-element.739) | copy-start | bytes 24580
  258.6 8.4 %copy-start.7 = (f32[3072,48]{1,0:T(8,128)S(1)}, f32[3072,48]{1,0:T(8,128)}, u32[]{:S(2)}) copy-start(f32[3072,48]{1,0:T(8,128)} %concatenate.42) | copy-start | bytes 1769476
  286.9 23.6 %copy-start.4 = (bf16[256,768]{1,0:T(8,128)(2,1)S(1)}, bf16[256,768]{1,0:T(8,128)(2,1)}, u32[]{:S(2)}) copy-start(bf16[256,768]{1,0:T(8,128)(2,1)} %param.24) | copy-start | bytes 1179652
  286.9 23.6 %copy-start.24 = (f32[768]{0:T(1024)S(1)}, f32[768]{0:T(1024)}, u32[]{:S(2)}) copy-start(f32[768]{0:T(1024)} %get-tuple-element.732) | copy-start | bytes 9220
  286.9 23.6 %copy-start.25 = (f32[768]{0:T(1024)S(1)}, f32[768]{0:T(1024)}, u32[]{:S(2)}) copy-start(f32[768]{0:T(1024)} %get-tuple-element.731) | copy-start | bytes 9220
  286.9 23.6 %copy-start.33 = (f32[256]{0:T(256)S(1)}, f32[256]{0:T(256)}, u32[]{:S(2)}) copy-start(f32[256]{0:T(256)} %copy-done.32) | copy-start | bytes 3076
  286.9 23.6 %copy-start.37 = (f32[256]{0:T(256)S(1)}, f32[256]{0:T(256)}, u32[]{:S(2)}) copy-start(f32[256]{0:T(256)} %copy-done.36) | copy-start | bytes 3076
  286.9 23.6 %copy-start.38 = (f32[3072]{0:T(1024)S(1)}, f32[3072]{0:T(1024)}, u32[]{:S(2)}) copy-start(f32[3072]{0:T(1024)} %slice.122) | copy-start | bytes 36868
  294.3 9.6 %copy-start = (f32[1024,3072]{1,0:T(8,128)S(1)}, f32[1024,3072]{1,0:T(8,128)}, u32[]{:S(2)}) copy-start(f32[1024,3072]{1,0:T(8,128)} %fusion.29) | copy-start | bytes 37748740 | tf_op jit(solution)/shard_map/while/body/eval_jaxpr/cond
  310.4 168.9 %reduce-scatter.8.cloned.1.call-start = ((), (), s32[]{:S(2)}) async-start(), calls=%async_computation.7 | async-start | bytes 7372800 | tf_op jit(solution)/shard_map/reduce_scatter | solution.py:297
  310.5 13.2 %copy-start.6 = (f32[3072,64]{0,1:T(8,128)S(1)}, f32[3072,64]{0,1:T(8,128)}, u32[]{:S(2)}) copy-start(f32[3072,64]{0,1:T(8,128)} %copy-done.5) | copy-start | bytes 2359300
  333.5 256.0 %reduce-scatter.6.cloned.1.call-start = ((), (), s32[]{:S(2)}) async-start(), calls=%async_computation.6 | async-start | bytes 7618560 | tf_op jit(solution)/shard_map/reduce_scatter | solution.py:294
  348.7 25.2 %copy-start.40 = (f32[256]{0:T(256)S(1)}, f32[256]{0:T(256)}, u32[]{:S(2)}) copy-start(f32[256]{0:T(256)} %copy-done.39) | copy-start | bytes 3076
  348.7 25.2 %copy-start.45 = (f32[8]{0:T(128)S(1)}, f32[8]{0:T(128)}, u32[]{:S(2)}) copy-start(f32[8]{0:T(128)} %copy-done.44) | copy-start | bytes 100
  348.7 26.1 %copy-start.35 = (f32[768]{0:T(1024)S(1)}, f32[768]{0:T(1024)}, u32[]{:S(2)}) copy-start(f32[768]{0:T(1024)} %copy-done.34) | copy-start | bytes 9220
  348.7 26.1 %copy-start.43 = (f32[768]{0:T(1024)S(1)}, f32[768]{0:T(1024)}, u32[]{:S(2)}) copy-start(f32[768]{0:T(1024)} %copy-done.42) | copy-start | bytes 9220
  392.1 62.4 %copy-start.23 = (f32[7808]{0:T(1024)S(1)}, f32[7808]{0:T(1024)}, u32[]{:S(2)}) copy-start(f32[7808]{0:T(1024)} %param.32) | copy-start | bytes 93700
  392.1 62.4 %copy-start.29 = (f32[7808]{0:T(1024)S(1)}, f32[7808]{0:T(1024)}, u32[]{:S(2)}) copy-start(f32[7808]{0:T(1024)} %param.34) | copy-start | bytes 93700
  392.1 62.4 %copy-start.30 = (f32[7808]{0:T(1024)S(1)}, f32[7808]{0:T(1024)}, u32[]{:S(2)}) copy-start(f32[7808]{0:T(1024)} %param.33) | copy-start | bytes 93700
  712.8 8.7 %copy-start.1 = (f32[960,768]{1,0:T(8,128)S(1)}, f32[960,768]{1,0:T(8,128)}, u32[]{:S(2)}) copy-start(f32[960,768]{1,0:T(8,128)} %param.29) | copy-start | bytes 8847364
  712.8 10.0 %copy-start.12 = (f32[960,768]{1,0:T(8,128)S(1)}, f32[960,768]{1,0:T(8,128)}, u32[]{:S(2)}) copy-start(f32[960,768]{1,0:T(8,128)} %param.31) | copy-start | bytes 8847364
  712.8 10.8 %copy-start.13 = (f32[960,768]{1,0:T(8,128)S(1)}, f32[960,768]{1,0:T(8,128)}, u32[]{:S(2)}) copy-start(f32[960,768]{1,0:T(8,128)} %param.30) | copy-start | bytes 8847364
  (19 other events, 58.0 us)
Sparse Core Ops, SparseCore 0:
  10.5 111.5 all-gather.4
  124.2 110.3 all-gather.2
  310.5 62.4 reduce-scatter.3
  375.2 104.0 reduce-scatter.7
  481.4 108.0 reduce-scatter.5
where the time goes:
time: 743 us; the launch traced here: 735 us
  waiting for transfers between devices  364 us (49%)
  blocking collectives  197 us (27%)
  matrix products  67.6 us (9%)
  other arithmetic  44.9 us (6%)
  local copies, waits for them, and re-layouts  42.4 us (6%)
  between operations  15.4 us (2%)
    psum x1, blocking collectives, shards(): summed_in, summed_out = lax.psum((shard_in, shard_out), ('dp', 'ctx'))  123 us
    reduce_scatter x1, waiting for transfers between devices, shards(): lax.psum_scatter(grad_in.astype(jnp.bfloat16), 'head', scatter_dimension=...  110 us
    all_gather x1, waiting for transfers between devices, shards(): lax.all_gather(out_master.astype(jnp.bfloat16), 'head', axis=0, tiled=True)  105 us
    all_gather x1, waiting for transfers between devices, shards(): lax.all_gather(in_master.astype(jnp.bfloat16), 'head', axis=0, tiled=True)  105 us
    psum x1, blocking collectives, shards(): summed_vec = lax.psum(grad_vec, ('dp', 'head', 'ctx'))  58.5 us
    reduce_scatter x1, waiting for transfers between devices, shards(): lax.psum_scatter(grad_out.astype(jnp.bfloat16), 'head', scatter_dimension...  24.1 us
    reduce_scatter x1, waiting for transfers between devices, shards(): lax.psum_scatter(kv_terms, ('head', 'ctx'), scatter_dimension=0, tiled=True)  19.2 us
  transfers between devices with their start and end apart: 5, of which 5 were waited for; matrix products, arithmetic and copies ran while one was open for 10% of the time, Pallas kernels for 0%

commit v1 on v0

--- a/solution.py
+++ b/solution.py
@@ -1,6 +1,8 @@
 import jax
 import jax.numpy as jnp
 from jax import lax
+from jax.experimental import pallas as pl
+from jax.experimental.pallas import tpu as pltpu
 from jax.sharding import PartitionSpec as P
 
 HEADS = 12
@@ -326,6 +328,855 @@
     )
 
 
+MESH = pl.DeviceIdType.MESH
+F32 = jnp.float32
+BF16 = jnp.bfloat16
+HALF_HEADS = HEADS // 2
+VMEM_LIMIT = 60 * 1024 * 1024
+contract_plain = (((1,), (0,)), ((), ()))
+
+
+def vmem_specs(count):
+    return [pl.BlockSpec(memory_space=pltpu.VMEM)] * count
+
+
+def places():
+    z = lax.axis_index("head")
+    q = lax.axis_index("dp")
+    c = lax.axis_index("ctx")
+    qx = lax.rem(q, 2)
+    qy = q // 2
+    return z, q, c, qx, qy, qy * 2 + 1 - qx, (1 - qy) * 2 + qx
+
+
+def greet(partners):
+    barrier = pltpu.get_barrier_semaphore()
+    for partner in partners:
+        pl.semaphore_signal(barrier, inc=1, device_id=partner, device_id_type=MESH)
+    pl.semaphore_wait(barrier, len(partners))
+
+
+def remote(source, target, send_sem, recv_sem, device):
+    return pltpu.make_async_remote_copy(
+        src_ref=source,
+        dst_ref=target,
+        send_sem=send_sem,
+        recv_sem=recv_sem,
+        device_id=device,
+        device_id_type=MESH,
+    )
+
+
+def gather_kernel(
+    win, wout, tok, cot, all_in, all_out, all_tok, all_cot, send_sem, recv_sem, pair_send, pair_recv, local_sem
+):
+    z, q, c, qx, qy, xn, yn = places()
+    dg = (1 - qy) * 2 + 1 - qx
+    greet(
+        [(q, lax.rem(z + k, 4), c) for k in (1, 2, 3)]
+        + [(xn, z, c), (yn, z, c), (q, z, 1 - c)]
+    )
+    groups = ((0, 0, 512), (1, 0, 768), (0, 512, 2048))
+    own = (win, wout)
+    full = (all_in, all_out)
+
+    def span(group, part):
+        which, first, last = groups[group]
+        middle = (first + last) // 2
+        if part == 1:
+            return which, pl.ds(first, middle - first)
+        if part == 2:
+            return which, pl.ds(middle, last - middle)
+        return which, pl.ds(first, last - first)
+
+    def place(group, part, plane, quarter):
+        which, cols = span(group, part)
+        return full[which].at[plane, quarter, :, cols]
+
+    copies = []
+    for number, (source, target) in enumerate(((tok, all_tok), (cot, all_cot))):
+        copy = remote(source, target.at[c], pair_send.at[number], pair_recv.at[number], (q, z, 1 - c))
+        copy.start()
+        copies.append(copy)
+    steps = [(group, k) for group in range(3) for k in (1, 2, 3)]
+    for number, (group, k) in enumerate(steps):
+        which, cols = span(group, 0)
+        copy = remote(
+            own[which].at[q, :, cols],
+            place(group, 0, z, q),
+            send_sem.at[0, number],
+            recv_sem.at[0, number],
+            (q, lax.rem(z + k, 4), c),
+        )
+        copy.start()
+        copies.append(copy)
+    locals_ = [
+        pltpu.make_async_copy(win, all_in.at[z], local_sem.at[0]),
+        pltpu.make_async_copy(wout, all_out.at[z], local_sem.at[1]),
+        pltpu.make_async_copy(tok, all_tok.at[c], local_sem.at[2]),
+        pltpu.make_async_copy(cot, all_cot.at[c], local_sem.at[3]),
+    ]
+    for copy in locals_:
+        copy.start()
+
+    def landed(path, number, target):
+        remote(target, target, send_sem.at[path, number], recv_sem.at[path, number], (q, z, c)).wait_recv()
+
+    def spread(number):
+        group, k = steps[number]
+        plane = lax.rem(z + 4 - k, 4)
+        landed(0, number, place(group, 0, plane, q))
+        for path, device in ((1, (xn, z, c)), (2, (yn, z, c))):
+            piece = place(group, 0, plane, q)
+            copy = remote(piece, piece, send_sem.at[path, number], recv_sem.at[path, number], device)
+            copy.start()
+            copies.append(copy)
+
+    def relay(number):
+        group, k = steps[number]
+        plane = lax.rem(z + 4 - k, 4)
+        landed(1, number, place(group, 0, plane, xn))
+        piece = place(group, 1, plane, xn)
+        copy = remote(piece, piece, send_sem.at[3, number], recv_sem.at[3, number], (yn, z, c))
+        copy.start()
+        copies.append(copy)
+        landed(2, number, place(group, 0, plane, yn))
+        piece = place(group, 2, plane, yn)
+        copy = remote(piece, piece, send_sem.at[4, number], recv_sem.at[4, number], (xn, z, c))
+        copy.start()
+        copies.append(copy)
+
+    for number in range(len(steps)):
+        spread(number)
+        if number > 0:
+            relay(number - 1)
+    relay(len(steps) - 1)
+    for number, (group, k) in enumerate(steps):
+        plane = lax.rem(z + 4 - k, 4)
+        landed(3, number, place(group, 1, plane, dg))
+        landed(4, number, place(group, 2, plane, dg))
+    for number, target in enumerate((all_tok, all_cot)):
+        remote(
+            target.at[1 - c], target.at[1 - c], pair_send.at[number], pair_recv.at[number], (q, z, 1 - c)
+        ).wait_recv()
+    for copy in copies:
+        copy.wait_send()
+    for copy in locals_:
+        copy.wait()
+
+
+def gather_weights(win, wout, tok, cot):
+    rows_in, cols_in = win.shape[1:]
+    rows_out, cols_out = wout.shape[1:]
+    rows, width = tok.shape
+    return pl.pallas_call(
+        gather_kernel,
+        out_shape=(
+            jax.ShapeDtypeStruct((4, 4, rows_in, cols_in), BF16),
+            jax.ShapeDtypeStruct((4, 4, rows_out, cols_out), BF16),
+            jax.ShapeDtypeStruct((2, rows, width), BF16),
+            jax.ShapeDtypeStruct((2, rows, width), BF16),
+        ),
+        in_specs=vmem_specs(4),
+        out_specs=vmem_specs(4),
+        scratch_shapes=[
+            pltpu.SemaphoreType.DMA((5, 9)),
+            pltpu.SemaphoreType.DMA((5, 9)),
+            pltpu.SemaphoreType.DMA((2,)),
+            pltpu.SemaphoreType.DMA((2,)),
+            pltpu.SemaphoreType.DMA((4,)),
+        ],
+        compiler_params=pltpu.CompilerParams(
+            collective_id=0, has_side_effects=True, vmem_limit_bytes=VMEM_LIMIT
+        ),
+        name="gather_weights",
+    )(win, wout, tok, cot)
+
+
+BLOCK = 256
+
+
+def attention_kernel(
+    q_ref,
+    g_ref,
+    kv_ref,
+    att_ref,
+    dq_ref,
+    dkv_ref,
+    kv_all,
+    keys,
+    values,
+    keys_t,
+    values_t,
+    scores,
+    probs,
+    dkeys,
+    dvalues,
+    packed,
+    pair_in,
+    summed,
+    zone,
+    send_sem,
+    recv_sem,
+    local_sem,
+):
+    z, q, c, qx, qy, xn, yn = places()
+    greet([(q, lax.rem(z + k, 4), c) for k in (1, 2, 3)] + [(q, z, 1 - c)])
+    for k in (1, 2, 3):
+
+        @pl.when(z + k < 4)
+        def _():
+            remote(
+                kv_ref, kv_all.at[z], send_sem.at[0, k], recv_sem.at[0, k], (q, lax.rem(z + k, 4), c)
+            ).start()
+
+    dkeys[...] = jnp.zeros_like(dkeys)
+    dvalues[...] = jnp.zeros_like(dvalues)
+
+    def spread_block(block, index):
+        rows = pl.ds(pl.multiple_of(index * 512, 512), 512)
+        keys[rows, :] = block[:, :HEAD_DIM]
+        values[rows, :] = block[:, HEAD_DIM:]
+        turned = block.astype(F32).T.astype(BF16)
+        keys_t[:, rows] = turned[:HEAD_DIM]
+        values_t[:, rows] = turned[HEAD_DIM:]
+
+    spread_block(kv_ref[...], z)
+    for k in (1, 2, 3):
+
+        @pl.when(z - k >= 0)
+        def _():
+            source = lax.rem(z + 4 - k, 4)
+            remote(
+                kv_ref, kv_all.at[source], send_sem.at[0, k], recv_sem.at[0, k], (q, z, c)
+            ).wait_recv()
+            spread_block(kv_all[source], source)
+
+    def one(step, carry):
+        head = step // 2
+        half = lax.rem(step, 2)
+        dims = pl.ds(pl.multiple_of(head * HEAD_DIM, HEAD_DIM), HEAD_DIM)
+        cols = pl.ds(pl.multiple_of(half * BLOCK, BLOCK), BLOCK)
+        queries = q_ref[dims, cols]
+        grads = g_ref[dims, cols]
+        count = 2 * z + 1 + half
+        key_place = lax.broadcasted_iota(jnp.int32, (BLOCK, BLOCK), 0)
+        row_place = lax.broadcasted_iota(jnp.int32, (BLOCK, BLOCK), 1)
+
+        def rows_at(index):
+            return pl.ds(pl.multiple_of(index * BLOCK, BLOCK), BLOCK)
+
+        def score(index, top):
+            rows = rows_at(index)
+            part = jnp.dot(keys[rows, :], queries, preferred_element_type=F32)
+            hidden = (index - (count - 1)) * BLOCK + key_place > row_place
+            part = jnp.where(hidden, neg_fill, part)
+            scores[rows, :] = part
+            return jnp.maximum(top, jnp.max(part, axis=0, keepdims=True))
+
+        top = lax.fori_loop(0, count, score, jnp.full((1, BLOCK), neg_fill, F32))
+
+        def weigh(index, total):
+            rows = rows_at(index)
+            part = jnp.exp(scores[rows, :] - top)
+            scores[rows, :] = part
+            return total + jnp.sum(part, axis=0, keepdims=True)
+
+        total = lax.fori_loop(0, count, weigh, jnp.zeros((1, BLOCK), F32))
+        inverse = 1.0 / total
+
+        def attend_block(index, out):
+            rows = rows_at(index)
+            part = scores[rows, :] * inverse
+            scores[rows, :] = part
+            rounded = part.astype(BF16)
+            probs[rows, :] = rounded
+            return out + jnp.dot(values_t[:, rows], rounded, preferred_element_type=F32)
+
+        out = lax.fori_loop(0, count, attend_block, jnp.zeros((HEAD_DIM, BLOCK), F32))
+        att_ref[dims, cols] = out.astype(BF16)
+        inner = jnp.sum(grads.astype(F32) * out, axis=0, keepdims=True)
+
+        def back(index, dq):
+            rows = rows_at(index)
+            grad = jnp.dot(values[rows, :], grads, preferred_element_type=F32)
+            dscore = (scores[rows, :] * (grad - inner)).astype(BF16)
+            dkeys[rows, :] += lax.dot_general(
+                dscore, queries, contract_cols, preferred_element_type=F32
+            )
+            dvalues[rows, :] += lax.dot_general(
+                probs[rows, :], grads, contract_cols, preferred_element_type=F32
+            )
+            return dq + jnp.dot(keys_t[:, rows], dscore, preferred_element_type=F32)
+
+        dq_ref[dims, cols] = lax.fori_loop(0, count, back, jnp.zeros((HEAD_DIM, BLOCK), F32))
+        return carry
+
+    lax.fori_loop(0, 2 * HALF_HEADS, one, 0)
+
+    for index in range(4):
+        rows = pl.ds(index * 512, 512)
+        packed[index] = jnp.concatenate([dkeys[rows, :], dvalues[rows, :]], axis=1)
+    mine = pl.ds(pl.multiple_of(c * 256, 256), 256)
+    other = pl.ds(pl.multiple_of((1 - c) * 256, 256), 256)
+    pair = remote(
+        packed.at[:, other, :], pair_in, send_sem.at[1, 0], recv_sem.at[1, 0], (q, z, 1 - c)
+    )
+    pair.start()
+    pair.wait_recv()
+    for index in range(4):
+        summed[index] = packed[index, mine, :] + pair_in[index]
+    for k in (1, 2, 3):
+
+        @pl.when(z - k >= 0)
+        def _():
+            target = lax.rem(z + 4 - k, 4)
+            remote(
+                summed.at[target], zone.at[k - 1], send_sem.at[2, k], recv_sem.at[2, k], (q, target, c)
+            ).start()
+
+    dkv_ref[mine, :] = summed[z]
+    for k in (1, 2, 3):
+
+        @pl.when(z + k < 4)
+        def _():
+            remote(
+                zone.at[k - 1], zone.at[k - 1], send_sem.at[2, k], recv_sem.at[2, k], (q, z, c)
+            ).wait_recv()
+            dkv_ref[mine, :] += zone[k - 1]
+
+    last = remote(
+        dkv_ref.at[mine, :], dkv_ref.at[mine, :], send_sem.at[1, 1], recv_sem.at[1, 1], (q, z, 1 - c)
+    )
+    last.start()
+    remote(
+        dkv_ref.at[other, :], dkv_ref.at[other, :], send_sem.at[1, 1], recv_sem.at[1, 1], (q, z, 1 - c)
+    ).wait_recv()
+    last.wait_send()
+    pair.wait_send()
+    for k in (1, 2, 3):
+
+        @pl.when(z + k < 4)
+        def _():
+            remote(
+                kv_ref, kv_all.at[z], send_sem.at[0, k], recv_sem.at[0, k], (q, lax.rem(z + k, 4), c)
+            ).wait_send()
+
+        @pl.when(z - k >= 0)
+        def _():
+            target = lax.rem(z + 4 - k, 4)
+            remote(
+                summed.at[target], zone.at[k - 1], send_sem.at[2, k], recv_sem.at[2, k], (q, target, c)
+            ).wait_send()
+
+
+def attention(queries_t, grads_t, own_kv):
+    dims, rows = queries_t.shape
+    whole = 4 * rows
+    return pl.pallas_call(
+        attention_kernel,
+        out_shape=(
+            jax.ShapeDtypeStruct((dims, rows), BF16),
+            jax.ShapeDtypeStruct((dims, rows), F32),
+            jax.ShapeDtypeStruct((rows, 2 * HEAD_DIM), F32),
+        ),
+        in_specs=vmem_specs(3),
+        out_specs=vmem_specs(3),
+        scratch_shapes=[
+            pltpu.VMEM((4, rows, 2 * HEAD_DIM), BF16),
+            pltpu.VMEM((whole, HEAD_DIM), BF16),
+            pltpu.VMEM((whole, HEAD_DIM), BF16),
+            pltpu.VMEM((HEAD_DIM, whole), BF16),
+            pltpu.VMEM((HEAD_DIM, whole), BF16),
+            pltpu.VMEM((whole, BLOCK), F32),
+            pltpu.VMEM((whole, BLOCK), BF16),
+            pltpu.VMEM((whole, HEAD_DIM), F32),
+            pltpu.VMEM((whole, HEAD_DIM), F32),
+            pltpu.VMEM((4, rows, 2 * HEAD_DIM), F32),
+            pltpu.VMEM((4, rows // 2, 2 * HEAD_DIM), F32),
+            pltpu.VMEM((4, rows // 2, 2 * HEAD_DIM), F32),
+            pltpu.VMEM((3, rows // 2, 2 * HEAD_DIM), F32),
+            pltpu.SemaphoreType.DMA((3, 4)),
+            pltpu.SemaphoreType.DMA((3, 4)),
+            pltpu.SemaphoreType.DMA((2,)),
+        ],
+        compiler_params=pltpu.CompilerParams(
+            collective_id=1, has_side_effects=True, vmem_limit_bytes=VMEM_LIMIT
+        ),
+        name="attention",
+    )(queries_t, grads_t, own_kv)
+
+
+PLANE_ORDER = (2, 1, 3, 0)
+
+
+def reduce_kernel(
+    g_in,
+    g_out,
+    vec,
+    all_in,
+    all_out,
+    vec_sum,
+    x_in,
+    x_out,
+    y_in,
+    y_out,
+    ax_in,
+    ax_out,
+    ay_in,
+    ay_out,
+    bx_in,
+    bx_out,
+    by_in,
+    by_out,
+    t_in,
+    t_out,
+    z_in,
+    z_out,
+    own_in,
+    own_out,
+    vec_send,
+    vec_recv,
+    vec_zone,
+    send_sem,
+    recv_sem,
+    vec_send_sem,
+    vec_recv_sem,
+    last_send_sem,
+    last_recv_sem,
+    pair_send_sem,
+    pair_recv_sem,
+):
+    z, q, c, qx, qy, xn, yn = places()
+    dg = (1 - qy) * 2 + 1 - qx
+    to_x, to_y, to_pair = (xn, z, c), (yn, z, c), (q, z, 1 - c)
+    greet([(q, lax.rem(z + k, 4), c) for k in (1, 2, 3)] + [to_x, to_y, to_pair])
+    sent = []
+
+    def send(source, target, sems, index, device):
+        copy = remote(source, target, sems[0].at[index], sems[1].at[index], device)
+        copy.start()
+        sent.append(copy)
+
+    def landed(target, sems, index):
+        remote(target, target, sems[0].at[index], sems[1].at[index], to_pair).wait_recv()
+
+    main = (send_sem, recv_sem)
+    vecs = (vec_send_sem, vec_recv_sem)
+    lasts = (last_send_sem, last_recv_sem)
+    pairs = (pair_send_sem, pair_recv_sem)
+    grads = (g_in, g_out)
+    halves = tuple(ref.shape[-1] // 2 for ref in grads)
+    first = tuple(pl.ds(0, half) for half in halves)
+    second = tuple(pl.ds(half, half) for half in halves)
+    from_x, from_y = (x_in, x_out), (y_in, y_out)
+    ax, ay, bx, by = (ax_in, ax_out), (ay_in, ay_out), (bx_in, bx_out), (by_in, by_out)
+    totals, zones, own = (t_in, t_out), (z_in, z_out), (own_in, own_out)
+
+    def plane(step):
+        return lax.rem(z + PLANE_ORDER[step], 4)
+
+    def exchange(step):
+        h = plane(step)
+        for a in range(2):
+            send(grads[a].at[h, :, 1 - qx, :, first[a]], from_x[a].at[step], main, (step, 0, a), to_x)
+            send(grads[a].at[h, 1 - qy, :, :, second[a]], from_y[a].at[step], main, (step, 1, a), to_y)
+
+    def halve(step):
+        h = plane(step)
+        for a in range(2):
+            landed(from_x[a].at[step], main, (step, 0, a))
+            ax[a][step] = (
+                grads[a][h, 1 - qy, qx, :, first[a]].astype(F32) + from_x[a][step, 1 - qy].astype(F32)
+            ).astype(BF16)
+            send(ax[a].at[step], ay[a].at[step], main, (step, 2, a), to_y)
+            landed(from_y[a].at[step], main, (step, 1, a))
+            bx[a][step] = (
+                grads[a][h, qy, 1 - qx, :, second[a]].astype(F32) + from_y[a][step, 1 - qx].astype(F32)
+            ).astype(BF16)
+            send(bx[a].at[step], by[a].at[step], main, (step, 3, a), to_x)
+
+    def finish(step):
+        h = plane(step)
+        shift = PLANE_ORDER[step]
+        for a in range(2):
+            landed(ay[a].at[step], main, (step, 2, a))
+            left = (
+                grads[a][h, qy, qx, :, first[a]].astype(F32)
+                + from_x[a][step, qy].astype(F32)
+                + ay[a][step].astype(F32)
+            )
+            landed(by[a].at[step], main, (step, 3, a))
+            right = (
+                grads[a][h, qy, qx, :, second[a]].astype(F32)
+                + from_y[a][step, qx].astype(F32)
+                + by[a][step].astype(F32)
+            )
+            if shift == 0:
+                own[a][:, first[a]] = left
+                own[a][:, second[a]] = right
+            else:
+                totals[a][shift - 1, :, first[a]] = left.astype(BF16)
+                totals[a][shift - 1, :, second[a]] = right.astype(BF16)
+                send(
+                    totals[a].at[shift - 1],
+                    zones[a].at[shift - 1],
+                    main,
+                    (step, 4, a),
+                    (q, h, c),
+                )
+
+    send(vec, vec_recv.at[0], vecs, 0, to_x)
+    exchange(0)
+    exchange(1)
+    for step in range(4):
+        halve(step)
+        if step + 2 < 4:
+            exchange(step + 2)
+        if step < 3:
+            landed(vec_recv.at[step], vecs, step)
+            have = vec[...] if step == 0 else vec_send[step - 1]
+            vec_send[step] = have + vec_recv[step]
+            if step < 2:
+                send(vec_send.at[step], vec_recv.at[step + 1], vecs, step + 1, (to_y, to_pair)[step])
+            else:
+                for k in (1, 2, 3):
+                    send(
+                        vec_send.at[2], vec_zone.at[z], vecs, 2 + k, (q, lax.rem(z + k, 4), c)
+                    )
+                vec_zone[z] = vec_send[2]
+        if step > 0:
+            finish(step - 1)
+    finish(3)
+    for step in range(3):
+        shift = PLANE_ORDER[step]
+        for a in range(2):
+            landed(zones[a].at[shift - 1], main, (step, 4, a))
+    outs = (all_in, all_out)
+    for a in range(2):
+        whole = own[a][...] + zones[a][0].astype(F32) + zones[a][1].astype(F32) + zones[a][2].astype(F32)
+        outs[a][c, q] = whole.astype(BF16)
+        piece = outs[a].at[c, q]
+        send(piece, piece, lasts, (0, a), to_x)
+        send(piece, piece, lasts, (1, a), to_y)
+        send(piece, piece, pairs, (0, a), to_pair)
+    for a in range(2):
+        piece = outs[a].at[c, xn]
+        landed(piece, lasts, (0, a))
+        part = outs[a].at[c, xn, :, first[a]]
+        send(part, part, lasts, (2, a), to_y)
+        send(piece, piece, pairs, (1, a), to_pair)
+        piece = outs[a].at[c, yn]
+        landed(piece, lasts, (1, a))
+        part = outs[a].at[c, yn, :, second[a]]
+        send(part, part, lasts, (3, a), to_x)
+        send(piece, piece, pairs, (2, a), to_pair)
+    for k in (1, 2, 3):
+        landed(vec_zone.at[lax.rem(z + 4 - k, 4)], vecs, 2 + k)
+    vec_sum[...] = (vec_zone[0] + vec_zone[1]) + (vec_zone[2] + vec_zone[3])
+    for a in range(2):
+        landed(outs[a].at[c, dg, :, first[a]], lasts, (2, a))
+        landed(outs[a].at[c, dg, :, second[a]], lasts, (3, a))
+        piece = outs[a].at[c, dg]
+        send(piece, piece, pairs, (3, a), to_pair)
+    for a in range(2):
+        for index, quarter in enumerate((q, xn, yn, dg)):
+            landed(outs[a].at[1 - c, quarter], pairs, (index, a))
+    for copy in sent:
+        copy.wait_send()
+
+
+def reduce_grads(grad_in, grad_out, vec):
+    rows_in, cols_in = grad_in.shape[3:]
+    rows_out, cols_out = grad_out.shape[3:]
+
+    def both(lead, cut, kind):
+        return [
+            pltpu.VMEM(lead + (rows_in, cols_in // cut), kind),
+            pltpu.VMEM(lead + (rows_out, cols_out // cut), kind),
+        ]
+
+    return pl.pallas_call(
+        reduce_kernel,
+        out_shape=(
+            jax.ShapeDtypeStruct((2, 4, rows_in, cols_in), BF16),
+            jax.ShapeDtypeStruct((2, 4, rows_out, cols_out), BF16),
+            jax.ShapeDtypeStruct(vec.shape, F32),
+        ),
+        in_specs=vmem_specs(3),
+        out_specs=vmem_specs(3),
+        scratch_shapes=both((4, 2), 2, BF16)
+        + both((4, 2), 2, BF16)
+        + both((4,), 2, BF16) * 4
+        + both((3,), 1, BF16) * 2
+        + both((), 1, F32)
+        + [
+            pltpu.VMEM((3,) + vec.shape, F32),
+            pltpu.VMEM((3,) + vec.shape, F32),
+            pltpu.VMEM((4,) + vec.shape, F32),
+            pltpu.SemaphoreType.DMA((4, 5, 2)),
+            pltpu.SemaphoreType.DMA((4, 5, 2)),
+            pltpu.SemaphoreType.DMA((6,)),
+            pltpu.SemaphoreType.DMA((6,)),
+            pltpu.SemaphoreType.DMA((4, 2)),
+            pltpu.SemaphoreType.DMA((4, 2)),
+            pltpu.SemaphoreType.DMA((4, 2)),
+            pltpu.SemaphoreType.DMA((4, 2)),
+        ],
+        compiler_params=pltpu.CompilerParams(
+            collective_id=2, has_side_effects=True, vmem_limit_bytes=VMEM_LIMIT
+        ),
+        name="reduce_grads",
+    )(grad_in, grad_out, vec)
+
+
+KV_END = D + 2 * HEAD_DIM
+HALF_D = D // 2
+
+
+def hidden_spans(core, ff, row_share):
+    spans = []
+    for owner in range((D + ff) // row_share):
+        first = max(owner * row_share - D, 0)
+        last = (owner + 1) * row_share - D
+        if last > first:
+            half = (last - first) // 2
+            spans.append((first + core * half, half))
+    return spans
+
+
+def core_columns(array, core, ff, row_share):
+    pieces = [array[..., core * HALF_D : (core + 1) * HALF_D], array[..., D:KV_END]]
+    pieces += [
+        array[..., KV_END + first : KV_END + first + size]
+        for first, size in hidden_spans(core, ff, row_share)
+    ]
+    return jnp.concatenate(pieces, axis=-1)
+
+
+def join_columns(pair, ff, row_share):
+    pieces = [pair[0][..., :HALF_D], pair[1][..., :HALF_D], pair[0][..., HALF_D : HALF_D + 2 * HEAD_DIM]]
+    at = HALF_D + 2 * HEAD_DIM
+    for _, size in hidden_spans(0, ff, row_share):
+        pieces += [pair[0][..., at : at + size], pair[1][..., at : at + size]]
+        at += size
+    return jnp.concatenate(pieces, axis=-1)
+
+
+def fast_shards(
+    tokens,
+    cotangent,
+    in_master,
+    in_moment,
+    in_second,
+    out_master,
+    out_moment,
+    out_second,
+    vec_master,
+    vec_moment,
+    vec_second,
+    rotary_scale,
+):
+    z = lax.axis_index("head")
+    c = lax.axis_index("ctx")
+    first_core = c == 0
+    rows = tokens.shape[0]
+    chip_rows = 2 * rows
+    row_share = out_master.shape[0]
+    ff = in_master.shape[1] - KV_END
+    half_share = row_share // 2
+    attn_share = D // 2
+
+    def pick(array):
+        return jnp.where(
+            first_core, core_columns(array, 0, ff, row_share), core_columns(array, 1, ff, row_share)
+        )
+
+    win = pick(in_master.astype(BF16))
+    out_low = out_master.astype(BF16)
+    start_one = jnp.where(z == 0, attn_share * c, half_share * c)
+    start_two = jnp.where(z == 0, D + (half_share - attn_share) * c, half_share * c + attn_share)
+    wout = jnp.concatenate(
+        [
+            lax.dynamic_slice_in_dim(out_low, start_one, attn_share, 0),
+            lax.dynamic_slice_in_dim(out_low, start_two, half_share - attn_share, 0),
+        ],
+        axis=0,
+    )
+    full_in, full_out, all_tok, all_cot = gather_weights(
+        win.reshape(4, -1, win.shape[1]), wout.reshape(4, -1, D), tokens, cotangent
+    )
+    full_in = full_in.reshape(D, -1)
+    full_out = full_out.reshape(-1, D)
+    inputs = all_tok.reshape(chip_rows, D).astype(F32)
+    cot = all_cot.reshape(chip_rows, D)
+    attn_cols = HALF_D + 2 * HEAD_DIM
+
+    gain_one, gain_two = vec_master[0:D], vec_master[2 * D : 3 * D]
+    center = inputs - jnp.mean(inputs, axis=-1, keepdims=True)
+    inverse = lax.rsqrt(jnp.mean(center * center, axis=-1, keepdims=True) + 1e-05)
+    normed = center * inverse
+    norm_one = (normed * gain_one + vec_master[D : 2 * D]).astype(BF16)
+    norm_two = (normed * gain_two + vec_master[3 * D : 4 * D]).astype(BF16)
+    bias = pick(vec_master[5 * D :])
+
+    positions = z * chip_rows + jnp.arange(chip_rows, dtype=jnp.int32)
+    cosine, sine_table = rotary_tables(
+        positions.astype(F32), rotary_scale[0].astype(F32)
+    )
+    half_rot = ROT // 2
+    cos_t, sin_t = cosine.T, sine_table.T
+
+    def turn(values, sine):
+        front, back = values[:, :half_rot], values[:, half_rot:ROT]
+        return jnp.concatenate(
+            [front * cos_t - back * sine, back * cos_t + front * sine, values[:, ROT:]], axis=1
+        )
+
+    projected = lax.dot_general(
+        full_in[:, :HALF_D], norm_one, (((0,), (1,)), ((), ())), preferred_element_type=F32
+    ) + bias[:HALF_D, None]
+    queries_t = (
+        (turn(projected.reshape(HALF_HEADS, HEAD_DIM, chip_rows), sin_t) * 0.125)
+        .astype(BF16)
+        .reshape(HALF_D, chip_rows)
+    )
+    shared = jnp.dot(norm_one, full_in[:, HALF_D:attn_cols], preferred_element_type=F32) + bias[
+        HALF_D:attn_cols
+    ]
+    own_kv = jnp.concatenate(
+        [rotate(shared[:, :HEAD_DIM], cosine, sine_table), shared[:, HEAD_DIM:]], axis=1
+    ).astype(BF16)
+    grads_t = lax.dot_general(
+        full_out[:HALF_D], cot, contract_cols, preferred_element_type=F32
+    ).astype(BF16)
+    att_t, query_grad, kv_grad = attention(queries_t, grads_t, own_kv)
+
+    hidden_in = jnp.dot(norm_two, full_in[:, attn_cols:], preferred_element_type=F32) + bias[attn_cols:]
+    activated = jax.nn.gelu(hidden_in, approximate=False).astype(BF16)
+    partial_out = lax.dot_general(
+        att_t, full_out[:HALF_D], contract_rows, preferred_element_type=F32
+    ) + jnp.dot(activated, full_out[HALF_D:], preferred_element_type=F32)
+    back_hidden = lax.dot_general(cot, full_out[HALF_D:], contract_cols, preferred_element_type=F32)
+    gelu_back = jax.vjp(lambda pre_act: jax.nn.gelu(pre_act, approximate=False), hidden_in)[1]
+    hidden_grad = gelu_back(back_hidden)[0].astype(BF16)
+    grad_out = jnp.concatenate(
+        [
+            jnp.dot(att_t, cot, preferred_element_type=F32).astype(BF16),
+            lax.dot_general(activated, cot, contract_rows, preferred_element_type=F32).astype(BF16),
+        ],
+        axis=0,
+    )
+    query_pre = (
+        turn(query_grad.reshape(HALF_HEADS, HEAD_DIM, chip_rows) * 0.125, -sin_t)
+        .reshape(HALF_D, chip_rows)
+        .astype(BF16)
+    )
+    shared_grad = jnp.concatenate(
+        [rotate(kv_grad[:, :HEAD_DIM], cosine, -sine_table), kv_grad[:, HEAD_DIM:]], axis=1
+    ).astype(BF16)
+    shared_once = jnp.where(first_core, shared_grad, jnp.zeros_like(shared_grad))
+    grad_in = jnp.concatenate(
+        [
+            lax.dot_general(
+                norm_one, query_pre, (((0,), (1,)), ((), ())), preferred_element_type=F32
+            ).astype(BF16),
+            lax.dot_general(norm_one, shared_grad, contract_rows, preferred_element_type=F32).astype(BF16),
+            lax.dot_general(norm_two, hidden_grad, contract_rows, preferred_element_type=F32).astype(BF16),
+        ],
+        axis=1,
+    )
+    norm_grad_one = lax.dot_general(
+        query_pre, full_in[:, :HALF_D], (((0,), (1,)), ((), ())), preferred_element_type=F32
+    ) + lax.dot_general(
+        shared_once, full_in[:, HALF_D:attn_cols], contract_cols, preferred_element_type=F32
+    )
+    norm_grad_two = lax.dot_general(
+        hidden_grad, full_in[:, attn_cols:], contract_cols, preferred_element_type=F32
+    )
+    upstream = norm_grad_one * gain_one + norm_grad_two * gain_two
+
+    def mine(array):
+        return lax.dynamic_slice_in_dim(array, c * rows, rows, 0)
+
+    def swap(array):
+        other = lax.dynamic_slice_in_dim(array, (1 - c) * rows, rows, 0)
+        return mine(array) + lax.ppermute(other, "ctx", [(0, 1), (1, 0)])
+
+    inputs_own = tokens.astype(F32)
+    cot_own = cotangent.astype(F32)
+    output = (inputs_own + swap(partial_out) + vec_master[4 * D : 5 * D]).astype(BF16)
+    upstream_own = swap(upstream)
+    normed_own = mine(normed)
+    inside = (
+        upstream_own
+        - jnp.mean(upstream_own, axis=-1, keepdims=True)
+        - normed_own * jnp.mean(upstream_own * normed_own, axis=-1, keepdims=True)
+    )
+    input_grad = (cot_own + mine(inverse) * inside).astype(BF16)
+
+    column_sums = jnp.concatenate(
+        [
+            jnp.sum(query_pre.astype(F32), axis=1),
+            jnp.sum(shared_once.astype(F32), axis=0),
+            jnp.sum(hidden_grad.astype(F32), axis=0),
+        ]
+    )
+    nothing = jnp.zeros_like(column_sums)
+    placed_sums = join_columns(
+        (jnp.where(first_core, column_sums, nothing), jnp.where(first_core, nothing, column_sums)),
+        ff,
+        row_share,
+    )
+    grad_vec = jnp.concatenate(
+        [
+            jnp.sum(norm_grad_one * normed, axis=0),
+            jnp.sum(norm_grad_one, axis=0),
+            jnp.sum(norm_grad_two * normed, axis=0),
+            jnp.sum(norm_grad_two, axis=0),
+            jnp.sum(cot_own, axis=0),
+            placed_sums,
+        ]
+    )
+    size = grad_vec.shape[0]
+    lanes = -(-size // 1024) * 128
+    padded = jnp.pad(grad_vec, (0, 8 * lanes - size)).reshape(8, lanes)
+    sum_in, sum_out, sum_vec = reduce_grads(
+        grad_in.reshape(4, 2, 2, -1, grad_in.shape[1]), grad_out.reshape(4, 2, 2, -1, D), padded
+    )
+    summed_vec = sum_vec.reshape(-1)[:size]
+    sum_in = sum_in.reshape(2, -1, sum_in.shape[-1])
+    summed_in = join_columns((sum_in[0], sum_in[1]), ff, row_share).astype(F32)
+    low, high = sum_out.reshape(2, half_share, D)
+    head_rows = jnp.concatenate([low[:attn_share], high[:attn_share], low[attn_share:], high[attn_share:]], axis=0)
+    summed_out = jnp.where(z == 0, head_rows, jnp.concatenate([low, high], axis=0)).astype(F32)
+
+    in_moment_new, in_second_new, in_master_new = adam_update(
+        in_master, in_moment, in_second, summed_in, matrix_rate, weight_decay
+    )
+    out_moment_new, out_second_new, out_master_new = adam_update(
+        out_master, out_moment, out_second, summed_out, matrix_rate, weight_decay
+    )
+    vec_moment_new, vec_second_new, vec_master_new = adam_update(
+        vec_master, vec_moment, vec_second, summed_vec, vector_rate, 0.0
+    )
+    return (
+        output,
+        input_grad,
+        in_moment_new,
+        in_second_new,
+        in_master_new,
+        in_master_new.astype(BF16),
+        out_moment_new,
+        out_second_new,
+        out_master_new,
+        out_master_new.astype(BF16),
+        vec_moment_new,
+        vec_second_new,
+        vec_master_new,
+    )
+
+
 def solution(mesh):
     placed = (
         P(("dp", "head", "ctx"), None),
@@ -341,8 +1192,10 @@
         P(),
         P(),
     )
+    paired = dict(mesh.shape) == {"dp": 4, "head": 4, "ctx": 2}
+    body = fast_shards if paired else shards
     return jax.shard_map(
-        shards,
+        body,
         mesh=mesh,
         in_specs=placed,
         out_specs=(

time: 743 us -> 361 us (0.49)
  waiting for transfers between devices: 364 us -> 0.01 us
  Pallas kernels: 0 us -> 250 us
  blocking collectives: 197 us -> 0 us
  matrix products: 67.6 us -> 34.9 us
  between operations: 15.4 us -> 2.19 us
  local copies, waits for them, and re-layouts: 42.4 us -> 32.8 us
    pallas_call x0 -> x3, Pallas kernels: none -> 250 us  [the longest x1 94.4 us: attention(): pl.pallas_call(attention_kernel, out_shape=(jax.ShapeDtypeStruct((dims, r...]
    all_gather x2 -> x0, waiting for transfers between devices: 210 us -> none  [the longest x1 105 us: shards(): lax.all_gather(out_master.astype(jnp.bfloat16), 'head', axis=0, tiled=True)]
    psum x2 -> x0, blocking collectives: 182 us -> none  [the longest x1 123 us: shards(): summed_in, summed_out = lax.psum((shard_in, shard_out), ('dp', 'ctx'))]
    reduce_scatter x3 -> x0, waiting for transfers between devices: 154 us -> none  [the longest x1 110 us: shards(): lax.psum_scatter(grad_in.astype(jnp.bfloat16), 'head', scatter_dimension=...]
    dot_general x16 -> x15, matrix products: 67.6 us -> 34.9 us  [the longest x1 8.44 us: fast_shards(): jnp.dot(norm_two, full_in[:, attn_cols:], preferred_element_type=F32)]
    all_gather x1 -> x0, blocking collectives: 14.8 us -> none  [shards(): whole_kv = lax.all_gather(shared, ('head', 'ctx'), axis=0, tiled=True)]
    slice x6 -> x36, local copies, waits for them, and re-layouts: 3.98 us -> 18.5 us  [the longest x5 3.95 us: join_columns(): pieces += [pair[0][..., at:at + size], pair[1][..., at:at + size]]]
    unnamed x93 -> x110, local copies, waits for them, and re-layouts: 10.3 us -> 2.78 us
  transfers between devices with their start and end apart: 5 -> 2, of which waited for: 5 -> 0; matrix products, arithmetic and copies ran while one was open for 10% -> 14% of each run, Pallas kernels for 0% -> 25%
where the time goes in v1:
time: 361 us; the launch traced here: 360 us
  Pallas kernels  250 us (69%)
  other arithmetic  40.1 us (11%)
  matrix products  34.9 us (10%)
  local copies, waits for them, and re-layouts  32.8 us (9%)
    pallas_call x1, Pallas kernels, attention(): pl.pallas_call(attention_kernel, out_shape=(jax.ShapeDtypeStruct((dims, r...  94.4 us
    pallas_call x1, Pallas kernels, reduce_grads(): pl.pallas_call(reduce_kernel, out_shape=(jax.ShapeDtypeStruct((2, 4, rows...  89.8 us
    pallas_call x1, Pallas kernels, gather_weights(): pl.pallas_call(gather_kernel, out_shape=(jax.ShapeDtypeStruct((4, 4, rows...  65.7 us
    dot_general x1, matrix products, fast_shards(): jnp.dot(norm_two, full_in[:, attn_cols:], preferred_element_type=F32)  8.44 us
    convert_element_type x1, other arithmetic, fast_shards(): in_master_new.astype(BF16)  7.9 us
  transfers between devices with their start and end apart: 2, of which 0 were waited for; matrix products, arithmetic and copies ran while one was open for 14% of the time, Pallas kernels for 25%

profile of v1, /device:TPU:0, one launch (start us, length us, event | category | flops | bytes accessed | tf_op | source)
XLA Modules:
  0.0 360.3 jit_solution(16424987729390978584)
XLA Ops:
  4.6 1.4 fusion.67
  6.0 2.2 convert_element_type.125
  8.3 1.4 fusion.63
  11.5 1.5 concatenate.91
  14.7 65.7 %gather_weights.1 = (bf16[4,4,48,2048]{3,2,1,0:T(8,128)(2,1)}, bf16[4,4,120,768]{3,2,1,0:T(8,128)(2,1)}, bf16[2,256,768]{2,1,0:T(8,128)(2,1)}, bf16[2,256,768]{2,1,0:T(8,128)(2,1)}) custom-call(bf16[4,48,2048]{2,1,0:T(8,128)(2,1)} %broadcast_select_fusion.win, bf16[4,120,768]{2,1,0:T(8,128)(2,1)} %bitcast.93, bf16[256,768]{1,0:T(8,128)(2,1)} %tok.1, ...), custom_call_target="tpu_custom_call" | custom-call | tf_op jit(solution)/shard_map/gather_weights/pallas_call | solution.py:472
  80.4 1.3 convert_reduce_fusion.1
  81.7 1.5 multiply_reduce_fusion.2
  83.8 2.5 add_convert_fusion.3
  86.3 1.4 convolution_add_fusion.4
  89.2 1.6 convolution_add_fusion.3
  90.9 2.3 convolution_convert_fusion.4.g_ref
  94.8 94.4 %attention.1 = (bf16[384,512]{1,0:T(8,128)(2,1)}, f32[384,512]{1,0:T(8,128)}, f32[512,128]{1,0:T(8,128)}) custom-call(bf16[384,512]{1,0:T(8,128)(2,1)} %bitcast.96, bf16[384,512]{1,0:T(8,128)(2,1)} %convolution_convert_fusion.4.g_ref, bf16[512,128]{1,0:T(8,128)(2,1)} %pad_maximum_fusion.3.kv_ref), custom_call_target="tpu_custom_call" | custom-call | tf_op jit(solution)/shard_map/attention/pallas_call | solution.py:676
  190.3 2.2 fusion.34
  194.5 1.3 fusion.41
  196.0 1.8 convolution_add_fusion.1
  198.1 8.4 %multiply_convert_fusion = (bf16[512,1536]{1,0:T(8,128)(2,1)S(1)}, f32[512,1536]{1,0:T(8,128)S(1)}, f32[512,1536]{1,0:T(8,128)S(1)}) fusion(f32[1536]{0:T(1024)S(1)} %slice.357, bf16[512,768]{1,0:T(8,128)(2,1)S(1)} %copy-done.26, bf16[768,2048]{1,0:T(8,128)(2,1)S(1)} %bitcast.113), kind=kOutput, calls=%fused_computation.12 | convolution fusion | flops 1259864064 | bytes 11018240 | tf_op jit(solution)/shard_map/dot_general | solution.py:1055
  206.6 3.1 convert_reduce_fusion
  209.7 3.5 fusion.54
  214.2 1.4 fusion.10
  218.6 1.3 convolution_convert_fusion.3
  219.9 2.8 convolution_convert_fusion
  223.2 1.3 convolution_convert_fusion.2
  224.5 3.6 %pad_maximum_fusion.1 = bf16[1920,768]{1,0:T(8,128)(2,1)} fusion(bf16[1536,768]{1,0:T(8,128)(2,1)} %convolution_convert_fusion, bf16[384,768]{1,0:T(8,128)(2,1)} %convolution_convert_fusion.3), kind=kLoop, calls=%fused_computation.29 | loop fusion | flops 5898240 | bytes 5898240 | tf_op jit(solution)/shard_map/concatenate | solution.py:1063
  231.1 1.4 copy.30
  232.7 3.1 convolution_convert_fusion.1
  235.8 2.0 pad_maximum_fusion
  240.1 89.8 %reduce_grads.1 = (bf16[2,4,48,2048]{3,2,1,0:T(8,128)(2,1)}, bf16[2,4,120,768]{3,2,1,0:T(8,128)(2,1)}, f32[8,1024]{1,0:T(8,128)}) custom-call(bf16[4,2,2,48,2048]{4,3,2,1,0:T(8,128)(2,1)} %bitcast.73, bf16[4,2,2,120,768]{4,3,2,1,0:T(8,128)(2,1)} %bitcast.74, f32[8,1024]{1,0:T(8,128)} %reshape.277.vec), custom_call_target="tpu_custom_call" | custom-call | tf_op jit(solution)/shard_map/reduce_grads/pallas_call | solution.py:899
  329.9 1.7 fusion.62
  339.6 3.7 %concatenate.103 = bf16[192,3968]{1,0:T(8,128)(2,1)} concatenate(bf16[192,384]{1,0:T(8,128)(2,1)} %slice.373, bf16[192,384]{1,0:T(8,128)(2,1)} %slice.374, bf16[192,224]{1,0:T(8,128)(2,1)S(1)} %slice.375, bf16[192,96]{1,0:T(8,128)(2,1)} %slice.376, bf16[192,480]{1,0:T(8,128)(2,1)} %get-tuple-element.81, bf16[192,480]{1,0:T(8,128)(2,1)} %get-tuple-element.78, ...), dimensions={1} | concatenate | bytes 3047424 | tf_op jit(solution)/shard_map/concatenate | solution.py:963
  343.3 7.9 %fusion.59 = (bf16[192,3968]{1,0:T(8,128)(2,1)}, f32[192,3968]{1,0:T(8,128)}, f32[192,3968]{1,0:T(8,128)}, f32[192,3968]{1,0:T(8,128)}) fusion(f32[192,3968]{1,0:T(8,128)S(1)} %copy-done.1, bf16[192,3968]{1,0:T(8,128)(2,1)} %concatenate.103, f32[192,3968]{1,0:T(8,128)} %param.16, f32[192,3968]{1,0:T(8,128)} %param.15), kind=kLoop, calls=%fused_computation.138 | loop fusion | flops 12189696 | bytes 21331968 | tf_op jit(solution)/shard_map/convert_element_type | solution.py:1169
  353.5 4.8 %fusion.57 = (bf16[960,768]{1,0:T(8,128)(2,1)}, f32[960,768]{1,0:T(8,128)}, f32[960,768]{1,0:T(8,128)}, f32[960,768]{1,0:T(8,128)}) fusion(f32[960,768]{1,0:T(8,128)S(1)} %copy-done.3, bf16[480,768]{1,0:T(8,128)(2,1)S(1)} %bitcast.83, bf16[480,768]{1,0:T(8,128)(2,1)S(1)} %bitcast.80, bf16[96,768]{1,0:T(8,128)(2,1)S(1)} %copy-done.28, ...), kind=kLoop, calls=%fused_computation.137 | loop fusion | flops 21381120 | bytes 22118400 | tf_op jit(solution)/shard_map/convert_element_type | solution.py:1173
  358.3 2.0 add_convert_fusion.4
  (188 shorter events, 34.0 us)
Async XLA Ops:
  4.6 5.1 %copy-start.33 = (f32[2048]{0:T(1024)}, f32[2048]{0:T(1024)S(1)}, u32[]{:S(2)}) copy-start(f32[2048]{0:T(1024)S(1)} %broadcast_select_fusion.3) | copy-start | bytes 24580
  6.0 4.3 %copy-start.2 = (f32[960,768]{1,0:T(8,128)S(1)}, f32[960,768]{1,0:T(8,128)}, u32[]{:S(2)}) copy-start(f32[960,768]{1,0:T(8,128)} %param.17) | copy-start | bytes 8847364
  80.4 8.8 %slice-start.3 = ((f32[2048]{0:T(1024)}), f32[384]{0:T(512)S(1)}, s32[]{:S(2)}) async-start(f32[2048]{0:T(1024)} %copy-done.33), calls=%async_computation.3 | async-start | bytes 4096 | tf_op jit(solution)/shard_map/slice | solution.py:1038
  86.3 4.5 %copy-start.22 = (bf16[2,256,768]{2,1,0:T(8,128)(2,1)S(1)}, bf16[2,256,768]{2,1,0:T(8,128)(2,1)}, u32[]{:S(2)}) copy-start(bf16[2,256,768]{2,1,0:T(8,128)(2,1)} %get-tuple-element.26) | copy-start | bytes 2359300
  198.1 8.5 %copy-start.23 = (bf16[2,256,768]{2,1,0:T(8,128)(2,1)S(1)}, bf16[2,256,768]{2,1,0:T(8,128)(2,1)}, u32[]{:S(2)}) copy-start(bf16[2,256,768]{2,1,0:T(8,128)(2,1)} %get-tuple-element.26) | copy-start | bytes 2359300
  198.1 8.5 %copy-start.32 = (bf16[4,4,120,768]{3,2,1,0:T(8,128)(2,1)S(1)}, bf16[4,4,120,768]{3,2,1,0:T(8,128)(2,1)}, u32[]{:S(2)}) copy-start(bf16[4,4,120,768]{3,2,1,0:T(8,128)(2,1)} %get-tuple-element.25) | copy-start | bytes 8847364
  209.7 3.5 copy-start.52
  214.1 23.8 %collective-permute-start.1 = (f32[256,768]{1,0:T(8,128)}, f32[256,768]{1,0:T(8,128)S(1)}, u32[]{:S(2)}, u32[]{:S(2)}) collective-permute-start(f32[256,768]{1,0:T(8,128)} %constant_dynamic-slice_fusion), channel_id=1, source_target_pairs={{0,1},{1,0},{2,3},{3,2},{4,5},{5,4},{6,7},{7,6},{8,9},{9,8},{10,11... | collective-permute-start | bytes 2359304 | tf_op jit(solution)/shard_map/ppermute | solution.py:1104
  217.3 141.0 %collective-permute-start = (f32[256,768]{1,0:T(8,128)}, f32[256,768]{1,0:T(8,128)}, u32[]{:S(2)}, u32[]{:S(2)}) collective-permute-start(f32[256,768]{1,0:T(8,128)} %constant_dynamic-slice_fusion.2), channel_id=1, source_target_pairs={{0,1},{1,0},{2,3},{3,2},{4,5},{5,4},{6,7},{7,6},{8,9},{9,8},{10,11... | collective-permute-start | bytes 2359304 | tf_op jit(solution)/shard_map/ppermute | solution.py:1104
  224.5 3.6 %copy-start.39 = (f32[1536]{0:T(1024)S(1)}, f32[1536]{0:T(1024)}, u32[]{:S(2)}) copy-start(f32[1536]{0:T(1024)} %get-tuple-element.116) | copy-start | bytes 18436
  224.5 3.6 %copy-start.50 = (f32[128]{0:T(128)S(1)}, f32[128]{0:T(128)}, u32[]{:S(2)}) copy-start(f32[128]{0:T(128)} %get-tuple-element.52) | copy-start | bytes 1540
  224.5 6.6 %copy-start.44 = (f32[1,1,2,256]{3,2,1,0:T(2,128)S(1)}, f32[1,1,2,256]{3,2,1,0:T(2,128)}, u32[]{:S(2)}) copy-start(f32[1,1,2,256]{3,2,1,0:T(2,128)} %get-tuple-element.112) | copy-start | bytes 6148
  224.5 8.0 %copy-start.27 = (bf16[768,128]{0,1:T(8,128)(2,1)S(1)}, bf16[768,128]{0,1:T(8,128)(2,1)}, u32[]{:S(2)}) copy-start(bf16[768,128]{0,1:T(8,128)(2,1)} %convolution_convert_fusion.5) | copy-start | bytes 589828
  329.8 5.8 %copy-start.19 = (bf16[2,4,120,768]{3,2,1,0:T(8,128)(2,1)S(1)}, bf16[2,4,120,768]{3,2,1,0:T(8,128)(2,1)}, u32[]{:S(2)}) copy-start(bf16[2,4,120,768]{3,2,1,0:T(8,128)(2,1)} %get-tuple-element.31) | copy-start | bytes 4423684
  335.6 3.3 copy-start.36
  335.6 3.3 copy-start.31
  335.6 3.3 copy-start.34
  335.6 3.3 copy-start.35
  335.8 3.1 copy-start.7
  336.5 6.7 %copy-start.1 = (f32[192,3968]{1,0:T(8,128)S(1)}, f32[192,3968]{1,0:T(8,128)}, u32[]{:S(2)}) copy-start(f32[192,3968]{1,0:T(8,128)} %param.14) | copy-start | bytes 9142276
  343.2 8.0 %copy-start.3 = (f32[960,768]{1,0:T(8,128)S(1)}, f32[960,768]{1,0:T(8,128)}, u32[]{:S(2)}) copy-start(f32[960,768]{1,0:T(8,128)} %param.17) | copy-start | bytes 8847364
  343.2 8.0 %copy-start.6 = (bf16[1,4,120,768]{3,2,1,0:T(8,128)(2,1)S(1)}, bf16[1,4,120,768]{3,2,1,0:T(8,128)(2,1)}, u32[]{:S(2)}) copy-start(bf16[1,4,120,768]{3,2,1,0:T(8,128)(2,1)} %copy-done.5) | copy-start | bytes 2211844
  343.2 8.0 %copy-start.8 = (bf16[1,4,120,768]{3,2,1,0:T(8,128)(2,1)S(1)}, bf16[1,4,120,768]{3,2,1,0:T(8,128)(2,1)}, u32[]{:S(2)}) copy-start(bf16[1,4,120,768]{3,2,1,0:T(8,128)(2,1)} %copy-done.7) | copy-start | bytes 2211844
  343.3 9.1 %copy-start.11 = (f32[960,768]{1,0:T(8,128)S(1)}, f32[960,768]{1,0:T(8,128)}, u32[]{:S(2)}) copy-start(f32[960,768]{1,0:T(8,128)} %param.19) | copy-start | bytes 8847364
  343.3 9.9 %copy-start.12 = (f32[960,768]{1,0:T(8,128)S(1)}, f32[960,768]{1,0:T(8,128)}, u32[]{:S(2)}) copy-start(f32[960,768]{1,0:T(8,128)} %param.18) | copy-start | bytes 8847364
  343.3 9.9 %copy-start.13 = (bf16[384,768]{1,0:T(8,128)(2,1)S(1)}, bf16[384,768]{1,0:T(8,128)(2,1)}, u32[]{:S(2)}) copy-start(bf16[384,768]{1,0:T(8,128)(2,1)} %slice.384) | copy-start | bytes 1769476
  343.3 10.1 %copy-start.14 = (bf16[384,768]{1,0:T(8,128)(2,1)S(1)}, bf16[384,768]{1,0:T(8,128)(2,1)}, u32[]{:S(2)}) copy-start(bf16[384,768]{1,0:T(8,128)(2,1)} %slice.383) | copy-start | bytes 1769476
  343.3 10.1 %copy-start.28 = (bf16[96,768]{1,0:T(8,128)(2,1)S(1)}, bf16[96,768]{1,0:T(8,128)(2,1)}, u32[]{:S(2)}) copy-start(bf16[96,768]{1,0:T(8,128)(2,1)} %slice.386) | copy-start | bytes 442372
  343.3 10.1 %copy-start.29 = (bf16[96,768]{1,0:T(8,128)(2,1)S(1)}, bf16[96,768]{1,0:T(8,128)(2,1)}, u32[]{:S(2)}) copy-start(bf16[96,768]{1,0:T(8,128)(2,1)} %slice.385) | copy-start | bytes 442372
  353.5 4.8 %copy-start.10 = (f32[512,768]{1,0:T(8,128)S(1)}, f32[512,768]{1,0:T(8,128)}, u32[]{:S(2)}) copy-start(f32[512,768]{1,0:T(8,128)} %copy-done.9) | copy-start | bytes 4718596
  353.5 4.9 %copy-start.17 = (bf16[256,768]{1,0:T(8,128)(2,1)S(1)}, bf16[256,768]{1,0:T(8,128)(2,1)}, u32[]{:S(2)}) copy-start(bf16[256,768]{1,0:T(8,128)(2,1)} %tok.1) | copy-start | bytes 1179652
  353.5 4.9 %copy-start.37 = (f32[768]{0:T(1024)S(1)}, f32[768]{0:T(1024)}, u32[]{:S(2)}) copy-start(f32[768]{0:T(1024)} %get-tuple-element.88) | copy-start | bytes 9220
  (27 other events, 50.8 us)
